TPU v7x, 512 devices: a whole 4x8x8 slice. The times are simulated.
512 devices in a mesh: dp: 64 (over z, y), member: 8 (over x, core).
Axes of the slice: x: 4, y: 8, z: 8, core: 2. Of those that a mesh axis runs over, the one named last changes fastest.
Arguments:
- inputs: bfloat16 [98304, 393], P(('dp', 'member')), may hold values from -256 to 256
- targets: bfloat16 [98304, 377], P(('dp', 'member')), may hold values from -6 to 6
- bootstrap: int32 [8, 98304], P('member', 'dp'), may hold values from 0 to 1535
- lower_weight: bfloat16 [8, 393, 1024], P('member'), may hold values from -0.3125 to 0.3125
- lower_shift: float32 [8, 1024], P('member'), may hold values from -3 to 3
- upper_weight: bfloat16 [8, 1024, 377], P('member'), may hold values from -0.1875 to 0.1875
- upper_shift: float32 [8, 377], P('member'), may hold values from -3 to 3
- log_var: float32 [8, 377], P('member'), may hold values from -1 to 1
Outputs:
- lower_grad: float32 [8, 1024, 393], P('member', 'dp')
- bias_grad: float32 [8, 1024], P('member', 'dp')
- upper_grad: float32 [8, 1024, 377], P('member', 'dp')
- offset_grad: float32 [8, 377], P('member')
- noise_grad: float32 [8, 377], P('member')
- member_loss: float32 [8], P('member')
Inputs may be any that keep to these rules, and one draw needn't show every extreme that they name: bootstrap[m, r] is an offset within the aligned block of 1536 rows that holds row r.
All inputs are finite; a program needn't handle non-finite values.
Results may differ from a plain program's by a relative error of at most 0.00076.
Values may be sent and summed in bfloat16 or wider, within the bound.
No kernel may reach another device: no remote copies, remote signals or barrier semaphores. Data moves between devices by JAX's collectives and lax.ppermute only.
A program may use at most 64 MiB of HBM per device.

v0:
```python
import jax
import jax.numpy as jnp
from jax import lax
from jax.sharding import Mesh
from jax.sharding import PartitionSpec as P

H = 1024
DP = ("dp_0", "dp_1")
MEMBER = ("member_0", "member_1")
DP_MEMBER = ("dp_0", "dp_1", "member_0", "member_1")


def over_axes(x, axes):
    for axis in axes:
        x = lax.psum(x, axis)
    return x


def sent_together(arrays, axis, dim, along):
    ends, at = ([], 0)
    for a in arrays[:-1]:
        at += a.shape[along]
        ends.append(at)
    both = jnp.concatenate(arrays, axis=along)
    return tuple(jnp.split(lax.all_gather(both, axis, axis=dim, tiled=True), ends, axis=along))


def split_up(x, dim, count):
    lengths = x.shape
    parts = x.reshape(*lengths[:dim], count, lengths[dim] // count, *lengths[dim + 1 :])
    return jnp.moveaxis(parts, dim, 0)


def summed_on_arrival(x, axis, dim):
    count = lax.axis_size(axis)
    parts = lax.all_to_all(split_up(x, dim, count), axis, 0, 0, tiled=True)
    return jnp.sum(parts, axis=0)


def summed_rows(total, axes):
    for axis in axes:
        total = lax.psum_scatter(total, axis, scatter_dimension=0, tiled=True)
    return total


def member_pass(
    picked, goal_rows, lower_weight, lower_shift, upper_weight, upper_shift, log_var, row_count
):
    pre_act = jnp.dot(picked, lower_weight, preferred_element_type=jnp.float32) + lower_shift
    hidden = jax.nn.silu(pre_act).astype(jnp.bfloat16)
    pred_mean = jnp.dot(hidden, upper_weight, preferred_element_type=jnp.float32) + upper_shift
    residual = pred_mean - goal_rows.astype(jnp.float32)
    scaled_err = residual * jnp.exp(-log_var)
    member_loss = 0.5 * jnp.sum(residual * scaled_err + log_var) / row_count
    grad_mean = scaled_err / row_count
    offset_grad = jnp.sum(grad_mean, axis=0)
    noise_grad = 0.5 * jnp.sum(1.0 - residual * scaled_err, axis=0) / row_count
    grad_half = grad_mean.astype(jnp.bfloat16)
    grad_hidden = lax.dot_general(
        grad_half, upper_weight, (((1,), (1,)), ((), ())), preferred_element_type=jnp.float32
    )
    gate_sig = jax.nn.sigmoid(pre_act)
    grad_pre = grad_hidden * gate_sig * (1.0 + pre_act * (1.0 - gate_sig))
    bias_grad = jnp.sum(grad_pre, axis=0)
    pre_half = grad_pre.astype(jnp.bfloat16)
    return (hidden, grad_half, pre_half, bias_grad, offset_grad, noise_grad, member_loss)


def outer_rows(left, right):
    return lax.dot_general(
        left, right, (((0,), (0,)), ((), ())), preferred_element_type=jnp.float32
    )


def feature_stats(inputs):
    values = inputs.astype(jnp.float32)
    row_count = inputs.shape[0] * lax.axis_size(DP) * lax.axis_size(MEMBER)
    col_total, col_squares = (
        over_axes(jnp.sum(values, axis=0), DP_MEMBER),
        over_axes(jnp.sum(values * values, axis=0), DP_MEMBER),
    )
    feature_mean = col_total / row_count
    feature_var = col_squares / row_count - feature_mean * feature_mean
    return (feature_mean, 1.0 / jnp.sqrt(feature_var + 1e-06))


def per_device(
    inputs, targets, bootstrap, lower_weight, lower_shift, upper_weight, upper_shift, log_var
):
    raw_block, goal_block = sent_together((inputs, targets), MEMBER, 0, 1)
    feature_mean, feature_scale = feature_stats(inputs)
    row_block = ((raw_block.astype(jnp.float32) - feature_mean) * feature_scale).astype(
        jnp.bfloat16
    )
    row_count = goal_block.shape[0]
    pick_row = bootstrap[0]
    picked = row_block[pick_row]
    passes = [
        (picked,)
        + member_pass(
            picked,
            goal_block[pick_row],
            lower_weight[0],
            lower_shift[0],
            upper_weight[0],
            upper_shift[0],
            log_var[0],
            row_count,
        )
    ]
    share = H // lax.axis_size(DP)
    lower_list, upper_list = ([], [])
    picked, hidden, grad_half, pre_half, bias_one, offset_one, noise_one, loss_one = passes[0]

    def upper_term(start, count, hidden=hidden, grad_half=grad_half):
        return outer_rows(hidden, grad_half)

    def lower_term(start, count, pre_half=pre_half, picked=picked):
        return outer_rows(pre_half, picked)

    upper_list.append(summed_on_arrival(upper_term(jnp.int32(0), share * lax.axis_size(DP)), DP, 0))
    lower_list.append(summed_rows(lower_term(jnp.int32(0), share * lax.axis_size(DP)), DP))
    lower_grad = jnp.stack(lower_list)
    upper_grad = jnp.stack(upper_list)
    bias_sum = jnp.stack([item[4] for item in passes])
    offset_sum = jnp.stack([item[5] for item in passes])
    noise_sum = jnp.stack([item[6] for item in passes])
    loss_sum = jnp.stack([item[7] for item in passes])
    bias_total, offset_grad, noise_grad, member_loss = (
        over_axes(bias_sum, DP),
        over_axes(offset_sum, DP),
        over_axes(noise_sum, DP),
        over_axes(loss_sum, DP),
    )
    bias_grad = lax.dynamic_slice_in_dim(bias_total, lax.axis_index(DP) * share, share, 1)
    return (lower_grad, bias_grad, upper_grad, offset_grad, noise_grad, member_loss)


def solution(mesh):
    finer = Mesh(mesh.devices.reshape(8, 8, 4, 2), ("dp_0", "dp_1", "member_0", "member_1"))
    return jax.shard_map(
        per_device,
        mesh=finer,
        in_specs=(
            P(DP_MEMBER, None),
            P(DP_MEMBER, None),
            P(MEMBER, DP),
            P(MEMBER, None, None),
            P(MEMBER, None),
            P(MEMBER, None, None),
            P(MEMBER, None),
            P(MEMBER, None),
        ),
        out_specs=(
            P(MEMBER, DP, None),
            P(MEMBER, DP),
            P(MEMBER, DP, None),
            P(MEMBER, None),
            P(MEMBER, None),
            P(MEMBER),
        ),
        check_vma=False,
    )
```

profile of v0, /device:TPU:2, one launch (start us, length us, event | category | flops | bytes accessed | tf_op | source)
XLA Modules:
  0.0 211.3 jit_solution(17410609025989401468)
XLA Ops:
  7.2 0.0 copy-start
  7.2 0.0 all-gather.2.cloned.1.call-start
  7.2 1.9 pad_maximum_fusion
  9.2 0.0 all-gather.2.cloned.1.call-update
  9.2 0.0 reduce-scatter.5.cloned.1.call-start
  9.2 0.7 reduce.1
  9.9 1.0 convert_reduce_fusion
  10.9 23.2 %all-reduce.3 = (f32[393]{0:T(512)S(1)}, f32[393]{0:T(512)S(1)}) all-reduce(f32[393]{0:T(512)S(1)} %get-tuple-element.28, f32[393]{0:T(512)S(1)} %get-tuple-element.27), channel_id=1, replica_groups=mesh['dp_0'=8,'dp_1'=8,'member_0'=4,'member_1'=2] {'dp_0'}, use_global_device_ids=true, to_apply=%region_6.0 | all-reduce | flops 786 | bytes 6288 | tf_op jit(solution)/shard_map/psum | solution.py:15
  34.1 17.6 %all-reduce.1 = (f32[393]{0:T(512)S(1)}, f32[393]{0:T(512)S(1)}) all-reduce(f32[393]{0:T(512)S(1)} %get-tuple-element.41, f32[393]{0:T(512)S(1)} %get-tuple-element.42), channel_id=1, replica_groups=mesh['dp_0'=8,'dp_1'=8,'member_0'=4,'member_1'=2] {'dp_1'}, use_global_device_ids=true, to_apply=%region_7.0 | all-reduce | flops 786 | bytes 6288 | tf_op jit(solution)/shard_map/psum | solution.py:15
  51.7 8.6 %all-reduce.4 = (f32[393]{0:T(512)S(1)}, f32[393]{0:T(512)S(1)}) all-reduce(f32[393]{0:T(512)S(1)} %get-tuple-element.35, f32[393]{0:T(512)S(1)} %get-tuple-element.36), channel_id=1, replica_groups=mesh['dp_0'=8,'dp_1'=8,'member_0'=4,'member_1'=2] {'member_0'}, use_global_device_ids=true, to_apply=%region_8.0 | all-reduce | flops 786 | bytes 6288 | tf_op jit(solution)/shard_map/psum | solution.py:15
  60.3 2.5 %all-reduce.5 = (f32[393]{0:T(512)S(1)}, f32[393]{0:T(512)S(1)}) all-reduce(f32[393]{0:T(512)S(1)} %get-tuple-element.43, f32[393]{0:T(512)S(1)} %get-tuple-element.44), channel_id=1, replica_groups=mesh['dp_0'=8,'dp_1'=8,'member_0'=4,'member_1'=2] {'member_1'}, use_global_device_ids=true, to_apply=%region_9.0 | all-reduce | flops 786 | bytes 6288 | tf_op jit(solution)/shard_map/psum | solution.py:15
  62.8 0.7 fusion.13
  63.5 0.7 fusion.16
  64.2 0.0 all-gather.2.cloned.1.call-done
  64.3 1.8 multiply_convert_fusion.1
  66.1 5.4 %gather_fusion = bf16[1536,393]{1,0:T(8,128)(2,1)} fusion(bf16[1536,393]{1,0:T(8,128)(2,1)S(1)} %multiply_convert_fusion.1, s32[2048]{0:T(1024)S(1)} %pad_clamp_fusion), kind=kCustom, calls=%fused_computation | custom fusion | bytes 2420736 | tf_op jit(solution)/shard_map/gather | solution.py:97
  71.5 1.9 split.9
  73.4 0.0 copy-start.3
  73.4 4.7 %gather_fusion.1 = bf16[1536,377]{1,0:T(8,128)(2,1)S(1)} fusion(bf16[1536,377]{1,0:T(8,128)(2,1)S(1)} %split.9, s32[2048]{0:T(1024)S(1)} %pad_clamp_fusion), kind=kCustom, calls=%fused_computation.1 | custom fusion | bytes 2322432 | tf_op jit(solution)/shard_map/gather | solution.py:102
  78.1 0.0 copy-done
  78.1 0.0 copy-done.3
  78.2 0.0 copy-start.2
  78.2 4.0 %multiply_convert_fusion = (bf16[1536,1024]{1,0:T(8,128)(2,1)S(1)}, f32[1536,1024]{1,0:T(8,128)S(1)}) fusion(f32[1024]{0:T(1024)S(1)} %bitcast.32, bf16[1536,393]{1,0:T(8,128)(2,1)} %gather_fusion, bf16[1,393,1024]{2,1,0:T(8,128)(2,1)S(1)} %copy-done), kind=kOutput, calls=%fused_computation.3 | convolution fusion | flops 1245708288 | bytes 11453440 | tf_op jit(solution)/shard_map/dot_general | solution.py:49
  82.2 0.0 copy-start.4
  82.2 0.0 copy-done.2
  82.2 3.2 %add_reduce_fusion = (f32[]{:T(128)}, f32[377]{0:T(512)S(1)}, f32[377]{0:T(512)S(1)}, f32[1536,377]{1,0:T(8,128)S(1)}) fusion(f32[377]{0:T(512)S(1)} %get-tuple-element.29, f32[377]{0:T(512)S(1)} %get-tuple-element.30, bf16[1536,377]{1,0:T(8,128)(2,1)S(1)} %gather_fusion.1, f32[377]{0:T(512)S(1)} %reduce.1, bf16[1536,1024]{1,0:T(8,128)(2,1)S(1)} %get-tuple-element.49, ...), kind=kOutput, calls=%fused_computation.12 | convolution fusion | flops 1192308480 | bytes 7399800 | tf_op jit(solution)/shard_map/dot_general | solution.py:51
  85.4 0.0 copy-done.4
  85.4 0.0 copy-start.5
  85.4 0.0 copy-start.1
  85.4 3.6 %fusion.17 = (f32[1024]{0:T(1024)S(1)}, bf16[1536,1024]{1,0:T(8,128)(2,1)S(1)}) fusion(f32[1536,1024]{1,0:T(8,128)S(1)} %get-tuple-element.50, f32[1024]{0:T(1024)S(1)} %bitcast.33, bf16[1,1024,377]{2,1,0:T(8,128)(2,1)S(1)} %copy-done.2, f32[1536,377]{1,0:T(8,128)S(1)} %get-tuple-element.53, f32[377]{0:T(512)S(1)} %get-tuple-element.30), kind=kOutput, calls=%fused_computation.36 | convolution fusion | flops 1204977152 | bytes 12535268 | tf_op jit(solution)/shard_map/dot_general | solution.py:59
  89.0 0.0 copy-done.5
  89.0 0.0 copy-done.1
  89.0 2.7 %fusion = f32[1024,393]{0,1:T(8,128)} fusion(bf16[1536,393]{1,0:T(8,128)(2,1)S(1)} %copy-done.1, bf16[1536,1024]{1,0:T(8,128)(2,1)S(1)} %get-tuple-element.52), kind=kOutput, calls=%fused_computation.7 | convolution fusion | flops 1236271104 | bytes 5962752 | tf_op jit(solution)/shard_map/dot_general | solution.py:70
  91.7 0.0 reduce-scatter.5.cloned.1.call-update
  91.8 5.7 %fusion.10 = f32[1024,377]{1,0:T(8,128)} fusion(bf16[1536,1024]{1,0:T(8,128)(2,1)} %copy-done.4, f32[1536,377]{1,0:T(8,128)} %copy-done.5, f32[377]{0:T(512)S(1)} %get-tuple-element.30), kind=kOutput, calls=%fused_computation.24 | convolution fusion | flops 1187676672 | bytes 7007716 | tf_op jit(solution)/shard_map/dot_general | solution.py:70
  97.4 6.2 %all-to-all-start = ((f32[64,16,377]{2,1,0:T(8,128)}), f32[64,16,377]{2,1,0:T(8,128)S(1)}, u32[]{:S(2)}, u32[]{:S(2)}) async-start(f32[64,16,377]{2,1,0:T(8,128)} %bitcast.28), calls=%async_computation.1 | async-start | bytes 3145728 | tf_op jit(solution)/shard_map/all_to_all | solution.py:36
  103.6 0.0 reduce-scatter.7.cloned.1.call-start
  103.7 58.3 %reduce-scatter.5.cloned.1.call-done = f32[128,393]{0,1:T(8,128)} async-done(((f32[1024,393]{0,1:T(8,128)}), f32[128,393]{0,1:T(8,128)}) %reduce-scatter.5.cloned.1.call-update) | async-done | bytes 201232 | tf_op jit(solution)/shard_map/reduce_scatter | solution.py:42
  161.9 1.8 copy.17
  163.7 0.0 reduce-scatter.7.cloned.1.call-update
  164.4 16.8 %all-reduce.2 = (f32[1,1024]{1,0:T(1,128)S(1)}, f32[1,377]{1,0:T(1,128)S(1)}, f32[1,377]{1,0:T(1,128)S(1)}, f32[1]{0:T(128)}) all-reduce(f32[1,1024]{1,0:T(1,128)S(1)} %bitcast.31, f32[1,377]{1,0:T(1,128)S(1)} %stack.19, f32[1,377]{1,0:T(1,128)S(1)} %div.37, ...), channel_id=1, replica_groups=mesh['dp_0'=8,'dp_1'=8,'member_0'=4,'member_1'=2] {'dp_0'}, use_global_device_ids=true, to_apply=%region_13.14 | all-reduce | flops 1779 | bytes 14232 | tf_op jit(solution)/shard_map/psum | solution.py:15
  181.2 18.1 %all-reduce = (f32[1,1024]{1,0:T(1,128)S(1)}, f32[1,377]{1,0:T(1,128)}, f32[1,377]{1,0:T(1,128)}, f32[1]{0:T(128)}) all-reduce(f32[1,1024]{1,0:T(1,128)S(1)} %get-tuple-element.37, f32[1,377]{1,0:T(1,128)S(1)} %get-tuple-element.38, ...), channel_id=1, replica_groups=mesh['dp_0'=8,'dp_1'=8,'member_0'=4,'member_1'=2] {'dp_1'}, use_global_device_ids=true, to_apply=%region_14.15 | all-reduce | flops 1779 | bytes 14232 | tf_op jit(solution)/shard_map/psum | solution.py:15
  199.3 0.6 constant_dynamic-slice_fusion
  199.8 0.0 all-to-all-done
  199.8 0.7 reduce_sum.66
  200.6 2.6 %reduce-scatter.7.cloned.1.call-done = f32[16,393]{1,0:T(8,128)} async-done(((f32[128,393]{1,0:T(8,128)}), f32[16,393]{1,0:T(8,128)}) %reduce-scatter.7.cloned.1.call-update) | async-done | bytes 25168
  203.1 0.9 copy.18
  204.0 0.7 copy.16
  (5 shorter events, 0.0 us)
Async XLA Ops:
  7.2 71.0 %copy-start = (bf16[1,393,1024]{2,1,0:T(8,128)(2,1)S(1)}, bf16[1,393,1024]{2,1,0:T(8,128)(2,1)}, u32[]{:S(2)}) copy-start(bf16[1,393,1024]{2,1,0:T(8,128)(2,1)} %param.11) | copy-start | bytes 2414596
  7.2 57.1 %all-gather.2.cloned.1.call-start = ((), (), s32[]{:S(2)}) async-start(), calls=%async_computation.3 | async-start | bytes 3096576 | tf_op jit(solution)/shard_map/all_gather | solution.py:25
  9.2 152.7 %reduce-scatter.5.cloned.1.call-start = ((), (), s32[]{:S(2)}) async-start(), calls=%async_computation.4 | async-start | bytes 1843200 | tf_op jit(solution)/shard_map/reduce_scatter | solution.py:42
  73.4 4.7 %copy-start.3 = (f32[1,1024]{1,0:T(1,128)S(1)}, f32[1,1024]{1,0:T(1,128)}, u32[]{:S(2)}) copy-start(f32[1,1024]{1,0:T(1,128)} %param.12) | copy-start | bytes 12292
  78.2 4.0 %copy-start.2 = (bf16[1,1024,377]{2,1,0:T(8,128)(2,1)S(1)}, bf16[1,1024,377]{2,1,0:T(8,128)(2,1)}, u32[]{:S(2)}) copy-start(bf16[1,1024,377]{2,1,0:T(8,128)(2,1)} %param.13) | copy-start | bytes 2316292
  82.2 3.2 %copy-start.4 = (bf16[1536,1024]{1,0:T(8,128)(2,1)}, bf16[1536,1024]{1,0:T(8,128)(2,1)S(1)}, u32[]{:S(2)}) copy-start(bf16[1536,1024]{1,0:T(8,128)(2,1)S(1)} %get-tuple-element.49) | copy-start | bytes 9437188
  85.4 3.6 %copy-start.5 = (f32[1536,377]{1,0:T(8,128)}, f32[1536,377]{1,0:T(8,128)S(1)}, u32[]{:S(2)}) copy-start(f32[1536,377]{1,0:T(8,128)S(1)} %get-tuple-element.53) | copy-start | bytes 6948868
  85.4 3.6 %copy-start.1 = (bf16[1536,393]{1,0:T(8,128)(2,1)S(1)}, bf16[1536,393]{1,0:T(8,128)(2,1)}, u32[]{:S(2)}) copy-start(bf16[1536,393]{1,0:T(8,128)(2,1)} %gather_fusion) | copy-start | bytes 3621892
  97.4 102.4 %all-to-all-start = ((f32[64,16,377]{2,1,0:T(8,128)}), f32[64,16,377]{2,1,0:T(8,128)S(1)}, u32[]{:S(2)}, u32[]{:S(2)}) async-start(f32[64,16,377]{2,1,0:T(8,128)} %bitcast.28), calls=%async_computation.1 | async-start | bytes 3145728 | tf_op jit(solution)/shard_map/all_to_all | solution.py:36
  103.6 99.5 %reduce-scatter.7.cloned.1.call-start = ((), (), s32[]{:S(2)}) async-start(), calls=%async_computation.5 | async-start | bytes 294912
Sparse Core Ops, SparseCore 0:
  10.1 35.4 all-gather.1
  91.9 70.0 reduce-scatter.4
  164.7 38.3 reduce-scatter.6
where the time goes:
time: 212 us; the launch traced here: 211 us
  blocking collectives  86.7 us (41%)
  waiting for transfers between devices  60.9 us (29%)
  matrix products  19.2 us (9%)
  local copies, waits for them, and re-layouts  16 us (8%)
  between operations  14.6 us (7%)
  other arithmetic  7.61 us (4%)
  starting transfers between devices  6.32 us (3%)
    psum x6, blocking collectives, over_axes(): x = lax.psum(x, axis)  86.7 us
    reduce_scatter x1, waiting for transfers between devices, summed_rows(): total = lax.psum_scatter(total, axis, scatter_dimension=0, tiled=True)  58.3 us
    dot_general x2, matrix products, outer_rows(): lax.dot_general(left, right, (((0,), (0,)), ((), ())), preferred_element_...  8.34 us
    all_to_all x1, starting transfers between devices, summed_on_arrival(): parts = lax.all_to_all(split_up(x, dim, count), axis, 0, 0, tiled=True)  6.2 us
    gather x1, local copies, waits for them, and re-layouts, per_device(): picked = row_block[pick_row]  5.43 us
    gather x1, local copies, waits for them, and re-layouts, per_device(): goal_block[pick_row]  4.71 us
  transfers between devices with their start and end apart: 4, of which 2 were waited for; matrix products, arithmetic and copies ran while one was open for 6% of the time, Pallas kernels for 0%

commit v1 on v0

--- a/solution.py
+++ b/solution.py
@@ -12,7 +12,7 @@
 
 def over_axes(x, axes):
     for axis in axes:
-        x = lax.psum(x, axis)
+        x = jnp.sum(lax.all_gather(x, axis), axis=0)
     return x
 
 

time: 212 us -> 332 us (1.57)
  the two profiles are of different devices: /device:TPU:2 before, /device:TPU:4 now
where the time goes in v1:
time: 332 us; the launch traced here: 331 us
  blocking collectives  191 us (58%)
  waiting for transfers between devices  58.3 us (18%)
  local copies, waits for them, and re-layouts  28.3 us (9%)
  matrix products  19.2 us (6%)
  between operations  18.6 us (6%)
  other arithmetic  9.17 us (3%)
  starting transfers between devices  6.53 us (2%)
    unnamed x6, blocking collectives  141 us
    reduce_scatter x1, waiting for transfers between devices, summed_rows(): total = lax.psum_scatter(total, axis, scatter_dimension=0, tiled=True)  58.3 us
    all_gather x2, blocking collectives, over_axes(): x = jnp.sum(lax.all_gather(x, axis), axis=0)  49.3 us
    unnamed x46, local copies, waits for them, and re-layouts  13.6 us
    dot_general x2, matrix products, outer_rows(): lax.dot_general(left, right, (((0,), (0,)), ((), ())), preferred_element_...  8.35 us
  transfers between devices with their start and end apart: 4, of which 1 were waited for; matrix products, arithmetic and copies ran while one was open for 8% of the time, Pallas kernels for 0%

profile of v1, /device:TPU:4, one launch (start us, length us, event | category | flops | bytes accessed | tf_op | source)
XLA Modules:
  0.0 330.9 jit_solution(3211646116791006577)
XLA Ops:
  7.2 1.9 pad_maximum_fusion
  9.2 1.3 dynamic-slice.4
  11.2 1.0 convert_reduce_fusion
  12.2 0.3 dynamic-update-slice
  12.5 0.3 dynamic-update-slice.4
  12.7 35.9 %all-reduce.17 = (f32[3144]{0:T(1024)S(1)}, f32[3144]{0:T(1024)S(1)}) all-reduce(f32[3144]{0:T(1024)S(1)} %dynamic-update-slice.4, f32[3144]{0:T(1024)S(1)} %dynamic-update-slice), channel_id=6, replica_groups=mesh['dp_0'=8,'dp_1'=8,'member_0'=4,'member_1'=2] {'dp_0'}, use_global_device_ids=true, to_apply=%add.4 | all-reduce | flops 6288 | bytes 50304
  48.7 1.3 dynamic-slice.5
  50.8 0.3 dynamic-update-slice.1
  51.1 0.3 dynamic-update-slice.5
  51.3 30.4 %all-reduce.15 = (f32[3144]{0:T(1024)S(1)}, f32[3144]{0:T(1024)S(1)}) all-reduce(f32[3144]{0:T(1024)S(1)} %dynamic-update-slice.5, f32[3144]{0:T(1024)S(1)} %dynamic-update-slice.1), channel_id=7, replica_groups=mesh['dp_0'=8,'dp_1'=8,'member_0'=4,'member_1'=2] {'dp_1'}, use_global_device_ids=true, to_apply=%add.5 | all-reduce | flops 6288 | bytes 50304
  81.8 1.3 dynamic-slice.6
  83.9 0.3 dynamic-update-slice.2
  84.1 0.3 dynamic-update-slice.6
  84.4 14.7 %all-reduce.18 = (f32[1572]{0:T(1024)S(1)}, f32[1572]{0:T(1024)S(1)}) all-reduce(f32[1572]{0:T(1024)S(1)} %dynamic-update-slice.6, f32[1572]{0:T(1024)S(1)} %dynamic-update-slice.2), channel_id=8, replica_groups=mesh['dp_0'=8,'dp_1'=8,'member_0'=4,'member_1'=2] {'member_0'}, use_global_device_ids=true, to_apply=%add.6 | all-reduce | flops 3144 | bytes 25152
  99.2 1.3 dynamic-slice.7
  101.7 2.5 all-reduce.19
  104.3 0.7 reduce.19
  105.0 0.7 fusion.13
  105.8 0.7 fusion.16
  106.5 1.8 multiply_convert_fusion.1
  108.3 5.4 %gather_fusion = bf16[1536,393]{1,0:T(8,128)(2,1)} fusion(bf16[1536,393]{1,0:T(8,128)(2,1)S(1)} %multiply_convert_fusion.1, s32[2048]{0:T(1024)S(1)} %pad_clamp_fusion), kind=kCustom, calls=%fused_computation | custom fusion | bytes 2420736 | tf_op jit(solution)/shard_map/gather | solution.py:97
  113.7 1.9 split.9
  115.7 4.7 %gather_fusion.1 = bf16[1536,377]{1,0:T(8,128)(2,1)S(1)} fusion(bf16[1536,377]{1,0:T(8,128)(2,1)S(1)} %split.9, s32[2048]{0:T(1024)S(1)} %pad_clamp_fusion), kind=kCustom, calls=%fused_computation.1 | custom fusion | bytes 2322432 | tf_op jit(solution)/shard_map/gather | solution.py:102
  120.4 4.0 %multiply_convert_fusion = (bf16[1536,1024]{1,0:T(8,128)(2,1)S(1)}, f32[1536,1024]{1,0:T(8,128)S(1)}) fusion(f32[1024]{0:T(1024)S(1)} %bitcast.42, bf16[1536,393]{1,0:T(8,128)(2,1)} %gather_fusion, bf16[1,393,1024]{2,1,0:T(8,128)(2,1)S(1)} %copy-done), kind=kOutput, calls=%fused_computation.3 | convolution fusion | flops 1245708288 | bytes 11453440 | tf_op jit(solution)/shard_map/dot_general | solution.py:49
  124.4 3.2 add_reduce_fusion
  127.6 3.6 %fusion.17 = (f32[1024]{0:T(1024)S(1)}, bf16[1536,1024]{1,0:T(8,128)(2,1)S(1)}) fusion(f32[1536,1024]{1,0:T(8,128)S(1)} %get-tuple-element.54, f32[1024]{0:T(1024)S(1)} %bitcast.43, bf16[1,1024,377]{2,1,0:T(8,128)(2,1)S(1)} %copy-done.2, f32[1536,377]{1,0:T(8,128)S(1)} %get-tuple-element.57, f32[377]{0:T(512)S(1)} %get-tuple-element.36), kind=kOutput, calls=%fused_computation.36 | convolution fusion | flops 1204977152 | bytes 12535268 | tf_op jit(solution)/shard_map/dot_general | solution.py:59
  131.3 2.7 fusion
  134.0 5.7 %fusion.10 = f32[1024,377]{1,0:T(8,128)} fusion(bf16[1536,1024]{1,0:T(8,128)(2,1)} %copy-done.4, f32[1536,377]{1,0:T(8,128)} %copy-done.5, f32[377]{0:T(512)S(1)} %get-tuple-element.36), kind=kOutput, calls=%fused_computation.24 | convolution fusion | flops 1187676672 | bytes 7007716 | tf_op jit(solution)/shard_map/dot_general | solution.py:70
  139.7 6.4 %all-to-all-start = ((f32[64,16,377]{2,1,0:T(8,128)}), f32[64,16,377]{2,1,0:T(8,128)S(1)}, u32[]{:S(2)}, u32[]{:S(2)}) async-start(f32[64,16,377]{2,1,0:T(8,128)} %bitcast.39), calls=%async_computation.1 | async-start | bytes 3145728 | tf_op jit(solution)/shard_map/all_to_all | solution.py:36
  146.1 58.3 %reduce-scatter.5.cloned.1.call-done = f32[128,393]{0,1:T(8,128)} async-done(((f32[1024,393]{0,1:T(8,128)}), f32[128,393]{0,1:T(8,128)}) %reduce-scatter.5.cloned.1.call-update) | async-done | bytes 201232 | tf_op jit(solution)/shard_map/reduce_scatter | solution.py:42
  204.4 1.8 copy.18
  208.1 0.3 dynamic-update-slice.8
  208.4 0.8 dynamic-update-slice.12
  209.3 28.1 %all-reduce.16 = (f32[3016]{0:T(1024)S(1)}, f32[3016]{0:T(1024)S(1)}, f32[8]{0:T(128)S(1)}) all-reduce(f32[3016]{0:T(1024)S(1)} %dynamic-update-slice.8, f32[3016]{0:T(1024)S(1)} %multiply_dynamic-update-slice_fusion, f32[8]{0:T(128)S(1)} %dynamic-update-slice.12), channel_id=12, replica_groups=mesh['dp_0'=8,'dp_1'=8,'member_0'=4,'member_1'=2] {'dp_0'}, use_global_device_ids=true, to_apply=%add.8 | all-reduce | flops 6040 | bytes 48320
  237.6 0.3 dynamic-update-slice.11
  237.9 0.3 dynamic-update-slice.9
  238.1 0.6 reduce.14
  238.7 1.4 dynamic-update-slice.13
  240.2 29.9 %all-reduce.14 = (f32[3016]{0:T(1024)S(1)}, f32[3016]{0:T(1024)S(1)}, f32[8]{0:T(128)S(1)}) all-reduce(f32[3016]{0:T(1024)S(1)} %dynamic-update-slice.9, f32[3016]{0:T(1024)S(1)} %dynamic-update-slice.11, f32[8]{0:T(128)S(1)} %dynamic-update-slice.13), channel_id=13, replica_groups=mesh['dp_0'=8,'dp_1'=8,'member_0'=4,'member_1'=2] {'dp_1'}, use_global_device_ids=true, to_apply=%add.9 | all-reduce | flops 6040 | bytes 48320
  270.2 0.6 reduce_sum.230
  270.8 0.6 reduce_sum.234
  271.4 24.7 %all-gather.8 = f32[8192]{0:T(1024)S(1)} all-gather(f32[1024]{0:T(1024)S(1)} %get-tuple-element.55), channel_id=10, replica_groups=mesh['dp_0'=8,'dp_1'=8,'member_0'=4,'member_1'=2] {'dp_0'}, dimensions={0}, use_global_device_ids=true | all-gather | bytes 36864 | tf_op jit(solution)/shard_map/all_gather | solution.py:15
  296.1 24.7 %all-gather.9 = f32[8192]{0:T(1024)S(1)} all-gather(f32[1024]{0:T(1024)S(1)} %reduce.8), channel_id=11, replica_groups=mesh['dp_0'=8,'dp_1'=8,'member_0'=4,'member_1'=2] {'dp_1'}, dimensions={0}, use_global_device_ids=true | all-gather | bytes 36864 | tf_op jit(solution)/shard_map/all_gather | solution.py:15
  320.8 0.6 reduce.15
  321.4 0.6 dynamic-slice_bitcast_fusion
  322.0 0.7 reduce_sum.226
  322.7 0.9 copy.19
  323.6 0.7 copy.17
  (68 shorter events, 2.1 us)
Async XLA Ops:
  7.2 113.2 %copy-start = (bf16[1,393,1024]{2,1,0:T(8,128)(2,1)S(1)}, bf16[1,393,1024]{2,1,0:T(8,128)(2,1)}, u32[]{:S(2)}) copy-start(bf16[1,393,1024]{2,1,0:T(8,128)(2,1)} %param.11) | copy-start | bytes 2414596
  7.2 99.3 %all-gather.16.cloned.1.call-start = ((), (), s32[]{:S(2)}) async-start(), calls=%async_computation.3 | async-start | bytes 3096576 | tf_op jit(solution)/shard_map/all_gather | solution.py:25
  9.2 195.2 %reduce-scatter.5.cloned.1.call-start = ((), (), s32[]{:S(2)}) async-start(), calls=%async_computation.4 | async-start | bytes 1843200 | tf_op jit(solution)/shard_map/reduce_scatter | solution.py:42
  115.7 4.7 %copy-start.3 = (f32[1,1024]{1,0:T(1,128)S(1)}, f32[1,1024]{1,0:T(1,128)}, u32[]{:S(2)}) copy-start(f32[1,1024]{1,0:T(1,128)} %param.12) | copy-start | bytes 12292
  120.4 4.0 %copy-start.2 = (bf16[1,1024,377]{2,1,0:T(8,128)(2,1)S(1)}, bf16[1,1024,377]{2,1,0:T(8,128)(2,1)}, u32[]{:S(2)}) copy-start(bf16[1,1024,377]{2,1,0:T(8,128)(2,1)} %param.13) | copy-start | bytes 2316292
  124.4 3.2 copy-start.4
  127.6 3.6 %copy-start.5 = (f32[1536,377]{1,0:T(8,128)}, f32[1536,377]{1,0:T(8,128)S(1)}, u32[]{:S(2)}) copy-start(f32[1536,377]{1,0:T(8,128)S(1)} %get-tuple-element.57) | copy-start | bytes 6948868
  127.6 3.6 %copy-start.1 = (bf16[1536,393]{1,0:T(8,128)(2,1)S(1)}, bf16[1536,393]{1,0:T(8,128)(2,1)}, u32[]{:S(2)}) copy-start(bf16[1536,393]{1,0:T(8,128)(2,1)} %gather_fusion) | copy-start | bytes 3621892
  139.7 182.3 %all-to-all-start = ((f32[64,16,377]{2,1,0:T(8,128)}), f32[64,16,377]{2,1,0:T(8,128)S(1)}, u32[]{:S(2)}, u32[]{:S(2)}) async-start(f32[64,16,377]{2,1,0:T(8,128)} %bitcast.39), calls=%async_computation.1 | async-start | bytes 3145728 | tf_op jit(solution)/shard_map/all_to_all | solution.py:36
  146.1 176.6 %reduce-scatter.7.cloned.1.call-start = ((), (), s32[]{:S(2)}) async-start(), calls=%async_computation.5 | async-start | bytes 294912
Sparse Core Ops, SparseCore 0:
  10.1 35.3 all-gather.15
  134.1 70.2 reduce-scatter.4
  207.2 38.3 reduce-scatter.6
